TPU v7x, 32 devices: a whole 2x2x4 slice. The times are simulated.
32 devices in a mesh: rows: 8 (over y, x, core), sub: 4 (over z).
Axes of the slice: x: 2, y: 2, z: 4, core: 2. Of those that a mesh axis runs over, the one named last changes fastest.
Arguments:
- u_fem: float32 [120, 524288], P(None, ('rows', 'sub')), may hold values from -600 to 600
- resid_fem: float32 [1, 524288], P(None, ('rows', 'sub')), may hold values from -60 to 60
- slot_map: int32 [32, 32], P(('rows', 'sub')), may hold values from 0 to 31, as said below
- restart: float32 [120, 40], replicated, may hold values from -0.5 to 0.5
- coeff: float32 [3, 120, 120], P(None, None, 'sub'), may hold values from -6 to 6
Outputs:
- new_basis: float32 [40, 524288], P(None, ('rows', 'sub'))
- next_vector: float32 [1, 524288], P(None, ('rows', 'sub'))
- new_coeff: float32 [3, 40, 120], replicated
Inputs may be any that keep to these rules, and one draw needn't show every extreme that they name: Each row of slot_map is a permutation of 0 to 31.
All inputs are finite; a program needn't handle non-finite values.
Results may differ from a plain program's by a relative error of at most 0.00015.
Values sent between devices are 32-bit elements; how exact they have to be, the bound alone decides.
No kernel may reach another device: no remote copies, remote signals or barrier semaphores. Data moves between devices by JAX's collectives and lax.ppermute only.
A program may use at most 64 MiB of HBM per device.

v0:
```python
import jax
import jax.numpy as jnp
from jax import lax
from jax.sharding import PartitionSpec as P


def settle(values, source, dev_count):
    width = values.shape[0]
    block_len = values.shape[1] // dev_count
    blocks = values.reshape(width, dev_count, block_len)
    return jnp.take(blocks, source, axis=1).reshape(width, dev_count * block_len)


def local(u_fem, resid_fem, slot_map, restart, coeff):
    highest = lax.Precision.HIGHEST
    dev_count = lax.axis_size(("rows", "sub"))
    nrows_all = u_fem.shape[1] * dev_count
    source = jnp.argsort(slot_map[0])
    basis_rows, resid_row = (u_fem, resid_fem)
    gram_local = jnp.einsum("kn,jn->kj", basis_rows, basis_rows, precision=highest)
    inner_local = jnp.einsum("kn,n->k", basis_rows, resid_row[0], precision=highest)
    gram_sum = lax.psum(gram_local, ("rows", "sub"))
    chol_lower = jnp.linalg.cholesky(gram_sum / nrows_all)
    factor = lax.linalg.triangular_solve(
        chol_lower, restart, left_side=True, lower=True, transpose_a=True
    )
    new_rows = jnp.einsum("kp,kn->pn", factor, basis_rows, precision=highest)
    inner_prod = lax.psum(inner_local, ("rows", "sub"))
    half_solve = lax.linalg.triangular_solve(
        chol_lower, inner_prod[:, None], left_side=True, lower=True
    )
    proj_coef = (
        lax.linalg.triangular_solve(
            chol_lower, half_solve, left_side=True, lower=True, transpose_a=True
        )[:, 0]
        / nrows_all
    )
    remainder = resid_row - jnp.einsum("k,kn->n", proj_coef, basis_rows, precision=highest)[None, :]
    norm_sum = lax.psum(jnp.sum(remainder * remainder), ("rows", "sub"))
    next_row = remainder * lax.rsqrt(norm_sum / nrows_all + 1e-06)
    new_rows, next_row = (
        lax.all_to_all(new_rows, ("rows", "sub"), split_axis=1, concat_axis=1, tiled=True),
        lax.all_to_all(next_row, ("rows", "sub"), split_axis=1, concat_axis=1, tiled=True),
    )
    new_rows = settle(new_rows, source, dev_count)
    next_row = settle(next_row, source, dev_count)
    raised = jnp.dot(chol_lower, restart, precision=highest)
    coeff_all = lax.all_gather(coeff, "sub", axis=2, tiled=True)
    rotated = jnp.einsum("kp,ikm->ipm", raised, coeff_all, precision=highest)
    new_coeff = rotated * lax.rsqrt(jnp.mean(rotated * rotated) + 1e-06)
    return (new_rows, next_row, new_coeff)


def solution(mesh):
    in_specs = (
        P(None, ("rows", "sub")),
        P(None, ("rows", "sub")),
        P(("rows", "sub"), None),
        P(),
        P(None, None, "sub"),
    )
    out_specs = (P(None, ("rows", "sub")), P(None, ("rows", "sub")), P())
    return jax.shard_map(local, mesh=mesh, in_specs=in_specs, out_specs=out_specs, check_vma=False)
```

profile of v0, /device:TPU:0, one launch (start us, length us, event | category | flops | bytes accessed | tf_op | source)
XLA Modules:
  0.0 229.9 jit_solution(9403381852364649270)
XLA Ops:
  0.7 10.1 %fusion.16 = f32[120,120]{0,1:T(8,128)S(1)} fusion(f32[120,16384]{1,0:T(8,128)} %param.5), kind=kOutput, calls=%fused_computation.44 | convolution fusion | flops 2831155200 | bytes 7921920 | tf_op jit(solution)/shard_map/kn,jn->kj/dot_general | solution.py:20
  10.8 6.2 %convolution_bitcast_fusion.3 = f32[120]{0:T(128)S(1)} fusion(f32[120,16384]{1,0:T(8,128)S(1)} %copy-done.1, f32[1,16384]{1,0:T(1,128)S(1)} %copy-done.2), kind=kOutput, calls=%fused_computation.10 | convolution fusion | flops 23592960 | bytes 7930336 | tf_op jit(solution)/shard_map/kn,n->k/dot_general | solution.py:21
  16.9 42.8 %all-reduce = (f32[120,120]{0,1:T(8,128)S(1)}, f32[120]{0:T(128)S(1)}) all-reduce(f32[120,120]{0,1:T(8,128)S(1)} %fusion.16, f32[120]{0:T(128)S(1)} %convolution_bitcast_fusion.3), channel_id=1, replica_groups=mesh['rows'=8,'sub'=4] {'rows','sub'}, use_global_device_ids=true, to_apply=%region_1.2 | all-reduce | flops 14520 | bytes 116160 | tf_op jit(solution)/shard_map/psum | solution.py:22
  59.9 11.0 %cholesky.16 = f32[120,120]{1,0:T(8,128)S(1)} custom-call(f32[120,120]{1,0:T(8,128)S(1)} %fusion.9), custom_call_target="Cholesky" | custom-call | tf_op jit(solution)/shard_map/jit(cholesky)/cholesky | solution.py:23
  70.9 0.6 compare_reduce_fusion
  71.5 0.7 select_bitcast_fusion
  72.2 9.2 %custom-call.10 = f32[1,120,120]{1,2,0:T(8,128)S(1)} custom-call(f32[1,120,120]{2,1,0:T(8,128)S(1)} %select_bitcast_fusion), custom_call_target="InvertDiagBlocksLowerTriangular" | custom-call | tf_op jit(solution)/shard_map/triangular_solve | solution.py:24
  81.8 6.7 %multiply_reduce_fusion = (f32[]{:T(128)}, f32[1,16384]{1,0:T(1,128)S(1)}) fusion(f32[1,16384]{1,0:T(1,128)S(1)} %copy-done.2, f32[120,1]{0,1:T(1,128)S(1)} %fusion.1, f32[120,16384]{1,0:T(8,128)} %param.5), kind=kOutput, calls=%fused_computation.15 | convolution fusion | flops 23642112 | bytes 7995876 | tf_op jit(solution)/shard_map/k,kn->n/dot_general | solution.py:38
  88.5 40.3 %psum.23 = f32[]{:T(128)} all-reduce(f32[]{:T(128)} %get-tuple-element.7), channel_id=1, replica_groups=mesh['rows'=8,'sub'=4] {'rows','sub'}, use_global_device_ids=true, to_apply=%region_6.7 | all-reduce | flops 1 | bytes 8 | tf_op jit(solution)/shard_map/psum | solution.py:39
  129.5 0.7 broadcast_multiply_fusion
  130.1 5.4 %all-to-all-start.1 = ((f32[1,32,512]{2,0,1:T(1,128)}), f32[1,32,512]{2,0,1:T(1,128)S(1)}, u32[]{:S(2)}, u32[]{:S(2)}) async-start(f32[1,32,512]{2,0,1:T(1,128)} %bitcast.14), calls=%async_computation.1 | async-start | bytes 131072 | tf_op jit(solution)/shard_map/all_to_all | solution.py:43
  135.8 6.5 %fusion.17 = f32[40,16384]{1,0:T(8,128)S(1)} fusion(f32[120,40]{0,1:T(8,128)S(1)} %fusion.7, f32[120,16384]{1,0:T(8,128)} %param.5), kind=kOutput, calls=%fused_computation.45 | convolution fusion | flops 943718400 | bytes 10504960 | tf_op jit(solution)/shard_map/kp,kn->pn/dot_general | solution.py:27
  142.3 1.7 copy.36
  144.1 1.7 sort.17
  145.8 5.8 %all-to-all-start = ((f32[40,32,512]{2,0,1:T(8,128)}), f32[40,32,512]{2,0,1:T(8,128)S(1)}, u32[]{:S(2)}, u32[]{:S(2)}) async-start(f32[40,32,512]{2,0,1:T(8,128)} %bitcast.69), calls=%async_computation | async-start | bytes 5242880 | tf_op jit(solution)/shard_map/all_to_all | solution.py:42
  151.8 67.3 %all_gather.3 = f32[3,120,120]{1,0,2:T(4,128)S(1)} all-gather(f32[3,120,30]{1,0,2:T(4,128)S(1)} %copy.21), channel_id=1, replica_groups=mesh['rows'=8,'sub'=4] {'sub'}, dimensions={2}, use_global_device_ids=true | all-gather | bytes 216000 | tf_op jit(solution)/shard_map/all_gather | solution.py:48
  219.1 0.9 convolution_bitcast_fusion
  220.0 1.0 multiply_reduce_fusion.1
  221.9 0.6 multiply_bitcast_fusion
  222.5 0.6 gather_fusion.1
  223.2 0.7 broadcast_select_fusion.1
  223.9 2.2 gather_fusion
  226.2 2.1 copy.26
  228.2 1.7 broadcast_select_fusion
  (30 shorter events, 1.1 us)
Async XLA Ops:
  0.6 134.9 %copy-start = (f32[120,40]{0,1:T(8,128)S(1)}, f32[120,40]{0,1:T(8,128)}, u32[]{:S(2)}) copy-start(f32[120,40]{0,1:T(8,128)} %param.8) | copy-start | bytes 57604
  0.6 10.1 %copy-start.1 = (f32[120,16384]{1,0:T(8,128)S(1)}, f32[120,16384]{1,0:T(8,128)}, u32[]{:S(2)}) copy-start(f32[120,16384]{1,0:T(8,128)} %param.5) | copy-start | bytes 23592964
  0.7 10.1 %copy-start.2 = (f32[1,16384]{1,0:T(1,128)S(1)}, f32[1,16384]{1,0:T(1,128)}, u32[]{:S(2)}) copy-start(f32[1,16384]{1,0:T(1,128)} %param.6) | copy-start | bytes 196612
  130.1 15.6 %all-to-all-start.1 = ((f32[1,32,512]{2,0,1:T(1,128)}), f32[1,32,512]{2,0,1:T(1,128)S(1)}, u32[]{:S(2)}, u32[]{:S(2)}) async-start(f32[1,32,512]{2,0,1:T(1,128)} %bitcast.14), calls=%async_computation.1 | async-start | bytes 131072 | tf_op jit(solution)/shard_map/all_to_all | solution.py:43
  135.8 8.3 %copy-start.4 = (s32[1,32]{1,0:T(1,128)S(1)}, s32[1,32]{1,0:T(1,128)}, u32[]{:S(2)}) copy-start(s32[1,32]{1,0:T(1,128)} %param.7) | copy-start | bytes 388
  142.3 9.4 %copy-start.3 = (f32[3,120,30]{1,2,0:T(8,128)S(1)}, f32[3,120,30]{1,2,0:T(8,128)}, u32[]{:S(2)}) copy-start(f32[3,120,30]{1,2,0:T(8,128)} %param.9) | copy-start | bytes 129604
  145.8 78.2 %all-to-all-start = ((f32[40,32,512]{2,0,1:T(8,128)}), f32[40,32,512]{2,0,1:T(8,128)S(1)}, u32[]{:S(2)}, u32[]{:S(2)}) async-start(f32[40,32,512]{2,0,1:T(8,128)} %bitcast.69), calls=%async_computation | async-start | bytes 5242880 | tf_op jit(solution)/shard_map/all_to_all | solution.py:42
where the time goes:
time: 231 us; the launch traced here: 230 us
  blocking collectives  150 us (65%)
  matrix products  32 us (14%)
  other arithmetic  27 us (12%)
  starting transfers between devices  11.2 us (5%)
  local copies, waits for them, and re-layouts  7.06 us (3%)
    all_gather x1, blocking collectives, local(): coeff_all = lax.all_gather(coeff, 'sub', axis=2, tiled=True)  67.3 us
    psum x1, blocking collectives, local(): gram_sum = lax.psum(gram_local, ('rows', 'sub'))  42.8 us
    psum x1, blocking collectives, local(): norm_sum = lax.psum(jnp.sum(remainder * remainder), ('rows', 'sub'))  40.3 us
    another operation x3, other arithmetic, local(): chol_lower = jnp.linalg.cholesky(gram_sum / nrows_all)  11.6 us
    dot_general x1, matrix products, local(): jnp.einsum('kn,jn->kj', basis_rows, basis_rows, precision=highest)  10.1 us
    another operation x2, other arithmetic, local(): lax.linalg.triangular_solve(chol_lower, restart, left_side=True, lower=Tr...  9.85 us
    dot_general x1, matrix products, local(): jnp.einsum('k,kn->n', proj_coef, basis_rows, precision=highest)[None, :]  6.74 us
    dot_general x1, matrix products, local(): new_rows = jnp.einsum('kp,kn->pn', factor, basis_rows, precision=highest)  6.51 us
  transfers between devices with their start and end apart: 2, of which 0 were waited for; matrix products, arithmetic and copies ran while one was open for 6% of the time, Pallas kernels for 0%

commit v1 on v0

v1 whole, which is shorter than its diff:
```python
import functools

import jax
import jax.numpy as jnp
from jax import lax
from jax.experimental import pallas as pl
from jax.experimental.pallas import tpu as pltpu
from jax.sharding import PartitionSpec as P

AXES = ("rows", "sub")
LANES = 128
HIGH = lax.Precision.HIGHEST


def split(x):
    hi = x.astype(jnp.bfloat16)
    lo = (x - hi.astype(jnp.float32)).astype(jnp.bfloat16)
    return hi, lo


def augmented(u, r):
    pad = LANES - u.shape[0] - 1
    return jnp.concatenate([u, r, jnp.zeros((pad, u.shape[1]), jnp.float32)], axis=0)


def gram_body(u_ref, r_ref, out_ref, acc_ref):
    step = pl.program_id(0)
    both = jnp.concatenate(split(augmented(u_ref[...], r_ref[...])), axis=0)
    part = lax.dot_general(both, both, (((1,), (1,)), ((), ())), preferred_element_type=jnp.float32)

    @pl.when(step == 0)
    def _():
        acc_ref[...] = part

    @pl.when(step > 0)
    def _():
        acc_ref[...] += part

    @pl.when(step == pl.num_programs(0) - 1)
    def _():
        acc = acc_ref[...]
        out_ref[...] = (acc[:LANES, :LANES] + acc[LANES:, LANES:]) + (acc[:LANES, LANES:] + acc[LANES:, :LANES])


def gram_call(u, r, tile):
    k, n = u.shape
    return pl.pallas_call(
        gram_body,
        grid=(n // tile,),
        in_specs=[pl.BlockSpec((k, tile), lambda i: (0, i)), pl.BlockSpec((1, tile), lambda i: (0, i))],
        out_specs=pl.BlockSpec((LANES, LANES), lambda i: (0, 0)),
        out_shape=jax.ShapeDtypeStruct((LANES, LANES), jnp.float32),
        scratch_shapes=[pltpu.VMEM((2 * LANES, 2 * LANES), jnp.float32)],
        name="gram",
    )(u, r)


def dot_t(a, b):
    return lax.dot_general(a, b, (((0,), (0,)), ((), ())), precision=HIGH, preferred_element_type=jnp.float32)


def factor_body(s_ref, restart_ref, w_ref, raised_ref, *, k, nrows):
    keep = restart_ref.shape[1]
    row = lax.broadcasted_iota(jnp.int32, (LANES, LANES), 0)
    col = lax.broadcasted_iota(jnp.int32, (LANES, LANES), 1)
    s = s_ref[...]
    a = jnp.where((row < k) & (col < k), s * (1.0 / nrows), 0.0)
    inv = jnp.where(row == col, 1.0, 0.0).astype(jnp.float32)
    inner = s[k : k + 1, :] * (1.0 / nrows)
    low_t = []
    low_i = []
    for i in range(k):
        base = (i // 8) * 8
        off = i - i // 8 * 8
        pivot = a[off : off + 1, i : i + 1]
        scale = lax.rsqrt(pivot)
        scale = scale * (1.5 - 0.5 * pivot * scale * scale)
        urow = a[off : off + 1, :] * scale
        irow = inv[off : off + 1, :] * scale
        low_t.append(urow)
        low_i.append(irow)
        coef = a[:, i : i + 1] * scale
        a = a - coef * urow
        inv = inv - coef * irow
        if off == 7:
            a = a[8:, :]
            inv = inv[8:, :]
    zero = jnp.zeros((LANES - k, LANES), jnp.float32)
    low_t = jnp.concatenate(low_t + [zero], axis=0)
    low_i = jnp.concatenate(low_i + [zero], axis=0)
    low_t = jnp.where(col >= row, low_t, 0.0)
    low_i = jnp.where(col <= row, low_i, 0.0)
    restart = jnp.concatenate([restart_ref[...], jnp.zeros((LANES - k, keep), jnp.float32)], axis=0)
    factor_t = dot_t(restart, low_i)
    raised_ref[...] = dot_t(low_t, restart)
    half = jnp.sum(low_i * inner, axis=1, keepdims=True)
    proj = jnp.sum(low_i * half, axis=0, keepdims=True)
    lane = lax.broadcasted_iota(jnp.int32, (1, LANES), 1)
    last = jnp.where(lane < k, -proj, jnp.where(lane == k, 1.0, 0.0))
    pad = w_ref.shape[0] - keep - 1
    w_ref[...] = jnp.concatenate([factor_t, last, jnp.zeros((pad, LANES), jnp.float32)], axis=0)


def factor_call(s, restart, nrows, wrows):
    k, keep = restart.shape
    return pl.pallas_call(
        functools.partial(factor_body, k=k, nrows=nrows),
        out_shape=(
            jax.ShapeDtypeStruct((wrows, LANES), jnp.float32),
            jax.ShapeDtypeStruct((LANES, keep), jnp.float32),
        ),
        name="factor",
    )(s, restart)


def project_body(u_ref, r_ref, w_ref, out_ref, sum_ref, *, keep, block):
    step = pl.program_id(0)
    tile = u_ref.shape[1]
    per = tile // block
    chunks = block // LANES
    x = jnp.concatenate(split(augmented(u_ref[...], r_ref[...])), axis=0)
    whi, wlo = split(w_ref[...])
    w = jnp.concatenate([jnp.concatenate([whi, whi], axis=1), jnp.concatenate([wlo, wlo], axis=1)], axis=0)
    y = lax.dot_general(w, x, (((1,), (0,)), ((), ())), preferred_element_type=jnp.float32)
    half = w_ref.shape[0]
    y = y[:half] + y[half:]
    total = jnp.zeros((1, LANES), jnp.float32)
    for b in range(per):
        for c in range(chunks):
            lo = b * block + c * LANES
            out_ref[step * per + b, c * keep : (c + 1) * keep, :] = y[:keep, lo : lo + LANES]
            tail = y[keep : keep + 1, lo : lo + LANES]
            out_ref[step * per + b, chunks * keep + c : chunks * keep + c + 1, :] = tail
            total = total + tail * tail

    @pl.when(step == 0)
    def _():
        sum_ref[...] = total

    @pl.when(step > 0)
    def _():
        sum_ref[...] += total

    @pl.when(step == pl.num_programs(0) - 1)
    def _():
        first = chunks * (keep + 1)
        rest = out_ref.shape[1] - first
        out_ref[:, first:, :] = jnp.broadcast_to(sum_ref[...][None], (out_ref.shape[0], rest, LANES))


def project_call(u, r, w, ndev, keep, block, height, tile):
    k, n = u.shape
    return pl.pallas_call(
        functools.partial(project_body, keep=keep, block=block),
        grid=(n // tile,),
        in_specs=[
            pl.BlockSpec((k, tile), lambda i: (0, i)),
            pl.BlockSpec((1, tile), lambda i: (0, i)),
            pl.BlockSpec(w.shape, lambda i: (0, 0)),
        ],
        out_specs=pl.BlockSpec((ndev, height, LANES), lambda i: (0, 0, 0)),
        out_shape=jax.ShapeDtypeStruct((ndev, height, LANES), jnp.float32),
        scratch_shapes=[pltpu.VMEM((1, LANES), jnp.float32)],
        name="project",
    )(u, r, w)


def settle_body(slot_ref, got_ref, rows_ref, next_ref, *, keep, block, nrows):
    ndev = got_ref.shape[0]
    chunks = block // LANES
    first = chunks * (keep + 1)
    total = jnp.sum(got_ref[:, first, :])
    scale = lax.rsqrt(jnp.full((1, LANES), total / nrows + 1e-06, jnp.float32))

    def move(d, carry):
        start = pl.multiple_of(slot_ref[0, d] * block, block)
        for c in range(chunks):
            rows_ref[:, pl.ds(start + c * LANES, LANES)] = got_ref[d, c * keep : (c + 1) * keep, :]
            tail = got_ref[d, chunks * keep + c : chunks * keep + c + 1, :]
            next_ref[:, pl.ds(start + c * LANES, LANES)] = tail * scale
        return carry

    lax.fori_loop(0, ndev, move, 0)


def settle_call(slots, got, keep, block, nrows):
    n = got.shape[0] * block
    return pl.pallas_call(
        functools.partial(settle_body, keep=keep, block=block, nrows=nrows),
        in_specs=[pl.BlockSpec(memory_space=pltpu.SMEM), pl.BlockSpec(memory_space=pltpu.VMEM)],
        out_shape=(jax.ShapeDtypeStruct((keep, n), jnp.float32), jax.ShapeDtypeStruct((1, n), jnp.float32)),
        name="settle",
    )(slots, got)


def local(u_fem, resid_fem, slot_map, restart, coeff):
    ndev = lax.axis_size(AXES)
    nsub = lax.axis_size("sub")
    k, n = u_fem.shape
    keep = restart.shape[1]
    nrows = n * ndev
    block = n // ndev
    chunks = block // LANES
    tile = block * max(1, min(ndev, 2048 // block))

    coeff_all = lax.all_to_all(jnp.broadcast_to(coeff[None], (nsub,) + coeff.shape), "sub", 0, 0, tiled=True)
    gram = gram_call(u_fem, resid_fem, tile)
    per = -(-LANES // ndev)
    gram = jnp.pad(gram, ((0, per * ndev - LANES), (0, 0))).reshape(ndev, per, LANES)
    part = lax.all_to_all(gram, AXES, 0, 0, tiled=True).sum(axis=0, keepdims=True)
    whole = lax.all_to_all(jnp.broadcast_to(part, (ndev, per, LANES)), AXES, 0, 0, tiled=True)
    whole = whole.reshape(ndev * per, LANES)[:LANES]

    wrows = -(-(keep + 1) // 8) * 8
    w, raised = factor_call(whole, restart, float(nrows), wrows)
    height = -(-(chunks * (keep + 1) + 1) // 8) * 8
    sent = project_call(u_fem, resid_fem, w, ndev, keep, block, height, tile)
    got = lax.all_to_all(sent, AXES, 0, 0, tiled=True)
    new_rows, next_row = settle_call(slot_map, got, keep, block, float(nrows))

    coeff_all = jnp.moveaxis(coeff_all, 0, 2).reshape(coeff.shape[0], k, -1)
    rotated = jnp.einsum("kp,ikm->ipm", raised[:k], coeff_all, precision=HIGH)
    new_coeff = rotated * lax.rsqrt(jnp.mean(rotated * rotated) + 1e-06)
    return (new_rows, next_row, new_coeff)


def solution(mesh):
    in_specs = (
        P(None, AXES),
        P(None, AXES),
        P(AXES, None),
        P(),
        P(None, None, "sub"),
    )
    out_specs = (P(None, AXES), P(None, AXES), P())
    return jax.shard_map(local, mesh=mesh, in_specs=in_specs, out_specs=out_specs, check_vma=False)
```

time: 231 us -> 132 us (0.57)
  blocking collectives: 150 us -> 24.7 us
  waiting for transfers between devices: 0.01 us -> 59 us
  Pallas kernels: 0 us -> 32.9 us
  matrix products: 32 us -> 1.1 us
  other arithmetic: 27 us -> 0.67 us
  local copies, waits for them, and re-layouts: 7.06 us -> 3.02 us
  starting transfers between devices: 11.2 us -> 7.62 us
    psum x2 -> x0, blocking collectives: 83.1 us -> none  [the longest x1 42.8 us: local(): gram_sum = lax.psum(gram_local, ('rows', 'sub'))]
    all_gather x1 -> x0, blocking collectives: 67.3 us -> none  [local(): coeff_all = lax.all_gather(coeff, 'sub', axis=2, tiled=True)]
    all_to_all x2, waiting for transfers between devices: 0.01 us -> 59 us  [the longest x1 59 us: local(): got = lax.all_to_all(sent, AXES, 0, 0, tiled=True)]
    pallas_call x0 -> x4, Pallas kernels: none -> 32.9 us  [the longest x1 12.6 us: factor_call(): pl.pallas_call(functools.partial(factor_body, k=k, nrows=nrows), out_shap...]
    dot_general x6 -> x1, matrix products: 31.4 us -> 1.1 us  [local(): rotated = jnp.einsum('kp,ikm->ipm', raised[:k], coeff_all, precision=HIGH)]
    all_to_all x0 -> x2, blocking collectives: none -> 24.7 us  [the longest x1 14.8 us: local(): lax.all_to_all(gram, AXES, 0, 0, tiled=True).sum(axis=0, keepdims=True)]
    another operation x5 -> x0, other arithmetic: 21.5 us -> none  [the longest x3 11.6 us: local(): chol_lower = jnp.linalg.cholesky(gram_sum / nrows_all)]
    gather x3 -> x0, local copies, waits for them, and re-layouts: 4.86 us -> none  [settle(): jnp.take(blocks, source, axis=1).reshape(width, dev_count * block_len)]
  transfers between devices with their start and end apart: 2 -> 2, of which waited for: 0 -> 1; matrix products, arithmetic and copies ran while one was open for 6% -> 2% of each run, Pallas kernels for 0% -> 16%
where the time goes in v1:
time: 132 us; the launch traced here: 130 us
  waiting for transfers between devices  59 us (45%)
  Pallas kernels  32.9 us (25%)
  blocking collectives  24.7 us (19%)
  starting transfers between devices  7.62 us (6%)
  local copies, waits for them, and re-layouts  3.02 us (2%)
  between operations  1.39 us (1%)
    all_to_all x1, waiting for transfers between devices, local(): got = lax.all_to_all(sent, AXES, 0, 0, tiled=True)  59 us
    all_to_all x1, blocking collectives, local(): lax.all_to_all(gram, AXES, 0, 0, tiled=True).sum(axis=0, keepdims=True)  14.8 us
    pallas_call x1, Pallas kernels, factor_call(): pl.pallas_call(functools.partial(factor_body, k=k, nrows=nrows), out_shap...  12.6 us
    all_to_all x1, blocking collectives, local(): lax.all_to_all(jnp.broadcast_to(part, (ndev, per, LANES)), AXES, 0, 0, ti...  9.89 us
    pallas_call x1, Pallas kernels, project_call(): pl.pallas_call(functools.partial(project_body, keep=keep, block=block), g...  8.25 us
    pallas_call x1, Pallas kernels, gram_call(): pl.pallas_call(gram_body, grid=(n // tile,), in_specs=[pl.BlockSpec((k, t...  8.22 us
    all_to_all x1, starting transfers between devices, local(): got = lax.all_to_all(sent, AXES, 0, 0, tiled=True)  4.25 us
    pallas_call x1, Pallas kernels, settle_call(): pl.pallas_call(functools.partial(settle_body, keep=keep, block=block, nro...  3.85 us
  transfers between devices with their start and end apart: 2, of which 1 were waited for; matrix products, arithmetic and copies ran while one was open for 2% of the time, Pallas kernels for 16%

profile of v1, /device:TPU:0, one launch (start us, length us, event | category | flops | bytes accessed | tf_op | source)
XLA Modules:
  0.0 130.4 jit_solution(12518889898237109573)
XLA Ops:
  0.6 0.0 copy-start.2
  0.6 0.0 copy-start.3
  0.7 8.2 %gram.1 = f32[128,128]{1,0:T(8,128)} custom-call(f32[120,16384]{1,0:T(8,128)} %u_ref.3, f32[1,16384]{1,0:T(1,128)} %r_ref.3), custom_call_target="tpu_custom_call" | custom-call | tf_op jit(solution)/shard_map/gram/pallas_call | solution.py:47
  8.9 14.8 %all_to_all.20 = f32[32,4,128]{2,1,0:T(4,128)S(1)} all-to-all(f32[32,4,128]{2,1,0:T(4,128)} %bitcast.14), channel_id=1, replica_groups=mesh['rows'=8,'sub'=4] {'rows','sub'}, dimensions={0} | all-to-all | bytes 131072 | tf_op jit(solution)/shard_map/all_to_all | solution.py:210
  23.8 9.9 %all_to_all.21 = f32[32,4,128]{2,1,0:T(4,128)} all-to-all(f32[32,4,128]{2,1,0:T(4,128)S(1)} %broadcast_in_dim.4), channel_id=1, replica_groups=mesh['rows'=8,'sub'=4] {'rows','sub'}, dimensions={0} | all-to-all | bytes 131072 | tf_op jit(solution)/shard_map/all_to_all | solution.py:211
  33.6 0.0 copy-done.2
  33.7 0.7 broadcast_in_dim.5
  34.3 3.4 %all-to-all-start.3 = ((f32[4,3,120,30]{2,3,1,0:T(8,128)}), f32[4,3,120,30]{2,3,1,0:T(8,128)S(1)}, u32[]{:S(2)}, u32[]{:S(2)}) async-start(f32[4,3,120,30]{2,3,1,0:T(8,128)} %broadcast_in_dim.5), calls=%async_computation.3 | async-start | bytes 393216 | tf_op jit(solution)/shard_map/all_to_all | solution.py:206
  37.7 0.0 copy-done.3
  37.7 0.7 copy.14.restart_ref
  38.5 12.6 %factor.1 = (f32[48,128]{1,0:T(8,128)}, f32[128,40]{1,0:T(8,128)}) custom-call(f32[128,128]{1,0:T(8,128)} %bitcast.15, f32[120,40]{1,0:T(8,128)} %copy.14.restart_ref), custom_call_target="tpu_custom_call" | custom-call | tf_op jit(solution)/shard_map/factor/pallas_call | solution.py:106
  51.0 8.2 %project.1 = f32[32,168,128]{2,1,0:T(8,128)} custom-call(f32[120,16384]{1,0:T(8,128)} %u_ref.3, f32[1,16384]{1,0:T(1,128)} %r_ref.3, f32[48,128]{1,0:T(8,128)} %get-tuple-element.7.w_ref), custom_call_target="tpu_custom_call" | custom-call | tf_op jit(solution)/shard_map/project/pallas_call | solution.py:153
  59.3 0.0 copy-start.1
  59.3 0.0 all-to-all-done.3
  59.3 4.3 %all-to-all-start.2 = ((f32[32,168,128]{2,1,0:T(8,128)}), f32[32,168,128]{2,1,0:T(8,128)S(1)}, u32[]{:S(2)}, u32[]{:S(2)}) async-start(f32[32,168,128]{2,1,0:T(8,128)} %project.1), calls=%async_computation.2 | async-start | bytes 5505024 | tf_op jit(solution)/shard_map/all_to_all | solution.py:218
  63.6 0.0 copy-done.1
  63.6 1.1 multiply_reduce_fusion
  65.4 0.6 multiply_bitcast_fusion
  66.0 59.0 %all-to-all-done.2.got_ref = f32[32,168,128]{2,1,0:T(8,128)S(1)} async-done(((f32[32,168,128]{2,1,0:T(8,128)}), f32[32,168,128]{2,1,0:T(8,128)S(1)}, u32[]{:S(2)}, u32[]{:S(2)}) %all-to-all-start.2) | async-done | bytes 2752544 | tf_op jit(solution)/shard_map/all_to_all | solution.py:218
  125.0 0.0 copy-start
  125.0 1.5 %copy-done = f32[32,168,128]{2,1,0:T(8,128)} copy-done((f32[32,168,128]{2,1,0:T(8,128)}, f32[32,168,128]{2,1,0:T(8,128)S(1)}, u32[]{:S(2)}) %copy-start) | copy-done | bytes 2752536
  126.6 3.9 %settle.1 = (f32[40,16384]{1,0:T(8,128)}, f32[1,16384]{1,0:T(1,128)}) custom-call(s32[1,32]{1,0:T(1,128)} %slot_ref.1, f32[32,168,128]{2,1,0:T(8,128)} %copy-done), custom_call_target="tpu_custom_call" | custom-call | tf_op jit(solution)/shard_map/settle/pallas_call | solution.py:188
  (4 shorter events, 0.1 us)
Async XLA Ops:
  0.6 33.0 %copy-start.2 = (f32[3,120,30]{1,2,0:T(8,128)S(1)}, f32[3,120,30]{1,2,0:T(8,128)}, u32[]{:S(2)}) copy-start(f32[3,120,30]{1,2,0:T(8,128)} %param.9) | copy-start | bytes 129604
  0.6 37.1 %copy-start.3 = (f32[120,40]{0,1:T(8,128)S(1)}, f32[120,40]{0,1:T(8,128)}, u32[]{:S(2)}) copy-start(f32[120,40]{0,1:T(8,128)} %param.8) | copy-start | bytes 57604
  34.3 25.0 %all-to-all-start.3 = ((f32[4,3,120,30]{2,3,1,0:T(8,128)}), f32[4,3,120,30]{2,3,1,0:T(8,128)S(1)}, u32[]{:S(2)}, u32[]{:S(2)}) async-start(f32[4,3,120,30]{2,3,1,0:T(8,128)} %broadcast_in_dim.5), calls=%async_computation.3 | async-start | bytes 393216 | tf_op jit(solution)/shard_map/all_to_all | solution.py:206
  59.3 4.3 %copy-start.1 = (f32[128,40]{1,0:T(8,128)S(1)}, f32[128,40]{1,0:T(8,128)}, u32[]{:S(2)}) copy-start(f32[128,40]{1,0:T(8,128)} %get-tuple-element.10) | copy-start | bytes 61444
  59.3 65.7 %all-to-all-start.2 = ((f32[32,168,128]{2,1,0:T(8,128)}), f32[32,168,128]{2,1,0:T(8,128)S(1)}, u32[]{:S(2)}, u32[]{:S(2)}) async-start(f32[32,168,128]{2,1,0:T(8,128)} %project.1), calls=%async_computation.2 | async-start | bytes 5505024 | tf_op jit(solution)/shard_map/all_to_all | solution.py:218
  125.0 1.5 %copy-start = (f32[32,168,128]{2,1,0:T(8,128)}, f32[32,168,128]{2,1,0:T(8,128)S(1)}, u32[]{:S(2)}) copy-start(f32[32,168,128]{2,1,0:T(8,128)S(1)} %all-to-all-done.2.got_ref) | copy-start | bytes 8257540

commit v2 on v1

v2 whole, which is shorter than its diff:
```python
import functools

import jax
import jax.numpy as jnp
from jax import lax
from jax.experimental import pallas as pl
from jax.experimental.pallas import tpu as pltpu
from jax.sharding import PartitionSpec as P

AXES = ("rows", "sub")
LANES = 128
HIGH = lax.Precision.HIGHEST


def split(x):
    hi = x.astype(jnp.bfloat16)
    lo = (x - hi.astype(jnp.float32)).astype(jnp.bfloat16)
    return hi, lo


def augmented(u, r):
    pad = LANES - u.shape[0] - 1
    return jnp.concatenate([u, r, jnp.zeros((pad, u.shape[1]), jnp.float32)], axis=0)


def gram_body(u_hbm, r_hbm, out_ref, u_ref, r_ref, sems, *, tile):
    k, n = u_hbm.shape
    steps = n // tile

    def copy(i):
        cut = pl.ds(i * tile, tile)
        return pltpu.make_async_copy(u_hbm.at[:, cut], u_ref.at[:, cut], sems.at[i])

    rows = pltpu.make_async_copy(r_hbm, r_ref, sems.at[steps])
    rows.start()
    for i in range(steps):
        copy(i).start()
    rows.wait()
    acc = jnp.zeros((2 * LANES, 2 * LANES), jnp.float32)
    for i in range(steps):
        copy(i).wait()
        cut = pl.ds(i * tile, tile)
        both = jnp.concatenate(split(augmented(u_ref[:, cut], r_ref[:, cut])), axis=0)
        acc = acc + lax.dot_general(both, both, (((1,), (1,)), ((), ())), preferred_element_type=jnp.float32)
    out_ref[...] = (acc[:LANES, :LANES] + acc[LANES:, LANES:]) + (acc[:LANES, LANES:] + acc[LANES:, :LANES])


def gram_call(u, r, tile):
    k, n = u.shape
    far = pl.BlockSpec(memory_space=pltpu.HBM)
    return pl.pallas_call(
        functools.partial(gram_body, tile=tile),
        in_specs=[far, far],
        out_specs=pl.BlockSpec(memory_space=pltpu.VMEM),
        out_shape=pltpu.VMEM((LANES, LANES), jnp.float32),
        scratch_shapes=[
            pltpu.VMEM((k, n), jnp.float32),
            pltpu.VMEM((1, n), jnp.float32),
            pltpu.SemaphoreType.DMA((n // tile + 1,)),
        ],
        name="gram",
        compiler_params=pltpu.CompilerParams(vmem_limit_bytes=58 << 20),
    )(u, r)


def dot_t(a, b):
    return lax.dot_general(a, b, (((0,), (0,)), ((), ())), precision=HIGH, preferred_element_type=jnp.float32)


def root(pivot):
    scale = lax.rsqrt(pivot)
    return scale * (1.5 - 0.5 * pivot * scale * scale)


def update_body(
    s_ref, restart_ref, u_hbm, r_hbm, sent_hbm, raised_ref, u_ref, r_ref, sent_ref, in_sems, out_sems, *, nrows, block, tile
):
    k, n = u_hbm.shape
    keep = restart_ref.shape[1]
    steps = n // tile
    per = tile // block
    chunks = block // LANES
    body = chunks * keep

    def fetch(i):
        cut = pl.ds(i * tile, tile)
        return pltpu.make_async_copy(u_hbm.at[:, cut], u_ref.at[:, cut], in_sems.at[i])

    def ship(i):
        at = (pl.ds(i * per, per), pl.ds(0, body))
        return pltpu.make_async_copy(sent_ref.at[at], sent_hbm.at[at], out_sems.at[i])

    rows = pltpu.make_async_copy(r_hbm, r_ref, in_sems.at[steps])
    rows.start()
    for i in range(steps):
        fetch(i).start()
    row = lax.broadcasted_iota(jnp.int32, (LANES, LANES), 0)
    col = lax.broadcasted_iota(jnp.int32, (LANES, LANES), 1)
    s = s_ref[...]
    a = jnp.where((row < k) & (col < k), s * (1.0 / nrows), 0.0)
    inv = jnp.where(row == col, 1.0, 0.0).astype(jnp.float32)
    inner = s[k : k + 1, :] * (1.0 / nrows)
    low_t = []
    low_i = []
    for i in range(0, k, 2):
        off = i % 8
        col0 = jnp.broadcast_to(a[:, i : i + 1], a.shape)
        col1 = jnp.broadcast_to(a[:, i + 1 : i + 2], a.shape)
        scale0 = root(col0[off : off + 1])
        edge = col0[off + 1 : off + 2] * scale0
        scale1 = root(col1[off + 1 : off + 2] - edge * edge)
        urow0 = a[off : off + 1] * scale0
        urow1 = (a[off + 1 : off + 2] - edge * urow0) * scale1
        irow0 = inv[off : off + 1] * scale0
        irow1 = (inv[off + 1 : off + 2] - edge * irow0) * scale1
        low_t += [urow0, urow1]
        low_i += [irow0, irow1]
        col0 = col0 * scale0
        col1 = (col1 - col0 * edge) * scale1
        a = a - col0 * urow0 - col1 * urow1
        inv = inv - col0 * irow0 - col1 * irow1
        if off == 6:
            a = a[8:]
            inv = inv[8:]
    zero = jnp.zeros((LANES - k, LANES), jnp.float32)
    low_t = jnp.concatenate(low_t + [zero], axis=0)
    low_i = jnp.concatenate(low_i + [zero], axis=0)
    low_t = jnp.where(col >= row, low_t, 0.0)
    low_i = jnp.where(col <= row, low_i, 0.0)
    restart = jnp.concatenate([restart_ref[...], jnp.zeros((LANES - k, keep), jnp.float32)], axis=0)
    factor_t = dot_t(restart, low_i)
    raised_ref[...] = dot_t(low_t, restart)
    half = jnp.sum(low_i * inner, axis=1, keepdims=True)
    proj = jnp.sum(low_i * half, axis=0, keepdims=True)
    lane = lax.broadcasted_iota(jnp.int32, (1, LANES), 1)
    last = jnp.where(lane < k, -proj, jnp.where(lane == k, 1.0, 0.0))
    half = -(-(keep + 1) // 8) * 8
    pad = half - keep - 1
    w = jnp.concatenate([factor_t, last, jnp.zeros((pad, LANES), jnp.float32)], axis=0)
    whi, wlo = split(w)
    w = jnp.concatenate([jnp.concatenate([whi, whi], axis=1), jnp.concatenate([wlo, wlo], axis=1)], axis=0)

    rows.wait()
    total = jnp.zeros((1, LANES), jnp.float32)
    for i in range(steps):
        fetch(i).wait()
        cut = pl.ds(i * tile, tile)
        x = jnp.concatenate(split(augmented(u_ref[:, cut], r_ref[:, cut])), axis=0)
        y = lax.dot_general(w, x, (((1,), (0,)), ((), ())), preferred_element_type=jnp.float32)
        y = y[:half] + y[half:]
        for b in range(per):
            for c in range(chunks):
                lo = b * block + c * LANES
                sent_ref[i * per + b, c * keep : (c + 1) * keep, :] = y[:keep, lo : lo + LANES]
                tail = y[keep : keep + 1, lo : lo + LANES]
                sent_ref[i * per + b, body + c : body + c + 1, :] = tail
                total = total + tail * tail
        ship(i).start()
    first = body + chunks
    rest = sent_ref.shape[1] - first
    sent_ref[:, first:, :] = jnp.broadcast_to(total[None], (sent_ref.shape[0], rest, LANES))
    tails = pltpu.make_async_copy(sent_ref.at[:, body:, :], sent_hbm.at[:, body:, :], out_sems.at[steps])
    tails.start()
    for i in range(steps):
        ship(i).wait()
    tails.wait()


def update_call(s, restart, u, r, ndev, nrows, block, height, tile):
    k, keep = restart.shape
    n = u.shape[1]
    near = pl.BlockSpec(memory_space=pltpu.VMEM)
    far = pl.BlockSpec(memory_space=pltpu.HBM)
    return pl.pallas_call(
        functools.partial(update_body, nrows=nrows, block=block, tile=tile),
        in_specs=[near, near, far, far],
        out_specs=(far, near),
        out_shape=(pltpu.HBM((ndev, height, LANES), jnp.float32), pltpu.VMEM((LANES, keep), jnp.float32)),
        scratch_shapes=[
            pltpu.VMEM((k, n), jnp.float32),
            pltpu.VMEM((1, n), jnp.float32),
            pltpu.VMEM((ndev, height, LANES), jnp.float32),
            pltpu.SemaphoreType.DMA((n // tile + 1,)),
            pltpu.SemaphoreType.DMA((n // tile + 1,)),
        ],
        compiler_params=pltpu.CompilerParams(vmem_limit_bytes=58 << 20),
        name="update",
    )(s, restart, u, r)


def settle_body(slot_ref, got_ref, rows_ref, next_ref, tail_ref, sems, *, keep, block, nrows):
    ndev = got_ref.shape[0]
    chunks = block // LANES
    tails = pltpu.make_async_copy(got_ref.at[:, chunks * keep :, :], tail_ref, sems.at[0])
    tails.start()

    def move(d, carry):
        start = pl.multiple_of(slot_ref[0, d] * block, block)
        for c in range(chunks):
            pltpu.make_async_copy(
                got_ref.at[d, c * keep : (c + 1) * keep, :], rows_ref.at[:, pl.ds(start + c * LANES, LANES)], sems.at[1]
            ).start()
        return carry

    lax.fori_loop(0, ndev, move, 0)
    tails.wait()
    total = jnp.sum(tail_ref[:, chunks, :])
    scale = lax.rsqrt(jnp.full((1, LANES), total / nrows + 1e-06, jnp.float32))

    def place(d, carry):
        start = pl.multiple_of(slot_ref[0, d] * block, block)
        for c in range(chunks):
            next_ref[:, pl.ds(start + c * LANES, LANES)] = tail_ref[d, c : c + 1, :] * scale
        return carry

    lax.fori_loop(0, ndev, place, 0)
    pltpu.make_async_copy(rows_ref, rows_ref, sems.at[1]).wait()


def settle_call(slots, got, keep, block, nrows):
    ndev, height, _ = got.shape
    n = ndev * block
    chunks = block // LANES
    anywhere = pl.BlockSpec(memory_space=pl.ANY)
    return pl.pallas_call(
        functools.partial(settle_body, keep=keep, block=block, nrows=nrows),
        in_specs=[pl.BlockSpec(memory_space=pltpu.SMEM), anywhere],
        out_specs=(anywhere, pl.BlockSpec(memory_space=pltpu.VMEM)),
        out_shape=(jax.ShapeDtypeStruct((keep, n), jnp.float32), jax.ShapeDtypeStruct((1, n), jnp.float32)),
        scratch_shapes=[
            pltpu.VMEM((ndev, height - chunks * keep, LANES), jnp.float32),
            pltpu.SemaphoreType.DMA((2,)),
        ],
        name="settle",
        compiler_params=pltpu.CompilerParams(vmem_limit_bytes=12 << 20),
    )(slots, got)


def total_of(x, ndev):
    if ndev & (ndev - 1):
        return lax.psum(x, AXES)
    bit = 1
    while bit < ndev:
        x = x + lax.ppermute(x, AXES, [(i, i ^ bit) for i in range(ndev)])
        bit *= 2
    return x


def gather_sub(x):
    nsub = lax.axis_size("sub")
    turns = [x] + [lax.ppermute(x, "sub", [(i, (i + d) % nsub) for i in range(nsub)]) for d in range(1, nsub)]
    order = (lax.axis_index("sub") - jnp.arange(nsub)) % nsub
    picks = jax.nn.one_hot(order, nsub, dtype=jnp.bool_)
    return jnp.stack(
        [functools.reduce(lambda a, b: a + b, [jnp.where(picks[t, d], turns[d], 0.0) for d in range(nsub)]) for t in range(nsub)]
    )


def local(u_fem, resid_fem, slot_map, restart, coeff):
    ndev = lax.axis_size(AXES)
    k, n = u_fem.shape
    keep = restart.shape[1]
    nrows = n * ndev
    block = n // ndev
    chunks = block // LANES
    tile = block * max(1, min(ndev, 2048 // block))

    whole = total_of(gram_call(u_fem, resid_fem, tile), ndev)
    height = -(-(chunks * (keep + 1) + 1) // 8) * 8
    sent, raised = update_call(whole, restart, u_fem, resid_fem, ndev, float(nrows), block, height, tile)
    got = lax.all_to_all(sent, AXES, 0, 0, tiled=True)
    new_rows, next_row = settle_call(slot_map, got, keep, block, float(nrows))

    rotated = jnp.einsum("kp,ikm->ipm", raised[:k], coeff, precision=HIGH)
    rotated = jnp.moveaxis(gather_sub(rotated), 0, 2).reshape(coeff.shape[0], keep, -1)
    new_coeff = rotated * lax.rsqrt(jnp.mean(rotated * rotated) + 1e-06)
    return (new_rows, next_row, new_coeff)


def solution(mesh):
    in_specs = (
        P(None, AXES),
        P(None, AXES),
        P(AXES, None),
        P(),
        P(None, None, "sub"),
    )
    out_specs = (P(None, AXES), P(None, AXES), P())
    return jax.shard_map(local, mesh=mesh, in_specs=in_specs, out_specs=out_specs, check_vma=False)
```

time: 132 us -> 130 us (0.985)
  blocking collectives: 24.7 us -> 0 us
  starting transfers between devices: 7.62 us -> 22.5 us
  Pallas kernels: 32.9 us -> 20.6 us
  waiting for transfers between devices: 59 us -> 70.8 us
  other arithmetic: 0.67 us -> 11.6 us
    ppermute x0 -> x8, waiting for transfers between devices: none -> 70.8 us  [the longest x3 60.9 us: gather_sub(): lax.ppermute(x, 'sub', [(i, (i + d) % nsub) for i in range(nsub)])]
    all_to_all x1, waiting for transfers between devices: 59 us -> 0.01 us  [local(): got = lax.all_to_all(sent, AXES, 0, 0, tiled=True)]
    all_to_all x2 -> x0, blocking collectives: 24.7 us -> none  [the longest x1 14.8 us: local(): lax.all_to_all(gram, AXES, 0, 0, tiled=True).sum(axis=0, keepdims=True)]
    ppermute x0 -> x8, starting transfers between devices: none -> 15.7 us  [the longest x5 10.1 us: total_of(): x = x + lax.ppermute(x, AXES, [(i, i ^ bit) for i in range(ndev)])]
    pallas_call x3 -> x2, Pallas kernels: 29.1 us -> 18 us  [the longest x1 11.3 us: update_call(): pl.pallas_call(functools.partial(update_body, nrows=nrows, block=block, t...]
    another operation x0 -> x2, other arithmetic: none -> 10.1 us  [gather_sub(): jnp.stack([functools.reduce(lambda a, b: a + b, [jnp.where(picks[t, d], t...]
    all_to_all x1 -> x0, starting transfers between devices: 3.37 us -> none  [local(): lax.all_to_all(jnp.broadcast_to(coeff[None], (nsub,) + coeff.shape), 'sub...]
    all_to_all x1, starting transfers between devices: 4.25 us -> 6.77 us  [local(): got = lax.all_to_all(sent, AXES, 0, 0, tiled=True)]
  transfers between devices with their start and end apart: 2 -> 9, of which waited for: 1 -> 7; matrix products, arithmetic and copies ran while one was open for 2% -> 10% of each run, Pallas kernels for 16% -> 0%
where the time goes in v2:
time: 130 us; the launch traced here: 129 us
  waiting for transfers between devices  70.8 us (54%)
  starting transfers between devices  22.5 us (17%)
  Pallas kernels  20.6 us (16%)
  other arithmetic  11.6 us (9%)
  local copies, waits for them, and re-layouts  2.41 us (2%)
  between operations  1.44 us (1%)
    ppermute x3, waiting for transfers between devices, gather_sub(): lax.ppermute(x, 'sub', [(i, (i + d) % nsub) for i in range(nsub)])  60.9 us
    pallas_call x1, Pallas kernels, update_call(): pl.pallas_call(functools.partial(update_body, nrows=nrows, block=block, t...  11.3 us
    another operation x2, other arithmetic, gather_sub(): jnp.stack([functools.reduce(lambda a, b: a + b, [jnp.where(picks[t, d], t...  10.1 us
    ppermute x5, starting transfers between devices, total_of(): x = x + lax.ppermute(x, AXES, [(i, i ^ bit) for i in range(ndev)])  10.1 us
    ppermute x5, waiting for transfers between devices, total_of(): x = x + lax.ppermute(x, AXES, [(i, i ^ bit) for i in range(ndev)])  9.87 us
    all_to_all x1, starting transfers between devices, local(): got = lax.all_to_all(sent, AXES, 0, 0, tiled=True)  6.77 us
    pallas_call x1, Pallas kernels, gram_call(): pl.pallas_call(functools.partial(gram_body, tile=tile), in_specs=[far, fa...  6.66 us
    ppermute x3, starting transfers between devices, gather_sub(): lax.ppermute(x, 'sub', [(i, (i + d) % nsub) for i in range(nsub)])  5.65 us
  transfers between devices with their start and end apart: 9, of which 7 were waited for; matrix products, arithmetic and copies ran while one was open for 10% of the time, Pallas kernels for 0%

profile of v2, /device:TPU:0, one launch (start us, length us, event | category | flops | bytes accessed | tf_op | source)
XLA Modules:
  0.0 129.5 jit_solution(6460214922476268121)
XLA Ops:
  0.7 6.7 %gram.1 = f32[128,128]{1,0:T(8,128)S(1)} custom-call(f32[120,16384]{1,0:T(8,128)} %u_hbm.3, f32[1,16384]{1,0:T(1,128)} %r_hbm.3), custom_call_target="tpu_custom_call" | custom-call | tf_op jit(solution)/shard_map/gram/pallas_call | solution.py:51
  7.3 3.1 %collective-permute-start = (f32[128,128]{1,0:T(8,128)S(1)}, f32[128,128]{1,0:T(8,128)S(1)}, u32[]{:S(2)}, u32[]{:S(2)}) collective-permute-start(f32[128,128]{1,0:T(8,128)S(1)} %gram.1), channel_id=1, source_target_pairs={{0,1},{1,0},{2,3},{3,2},{4,5},{5,4},{6,7},{7,6},{8,9},{9,8},{10,11... | collective-permute-start | bytes 196616 | tf_op jit(solution)/shard_map/ppermute | solution.py:244
  10.4 2.2 %collective-permute-done = f32[128,128]{1,0:T(8,128)S(1)} collective-permute-done((f32[128,128]{1,0:T(8,128)S(1)}, f32[128,128]{1,0:T(8,128)S(1)}, u32[]{:S(2)}, u32[]{:S(2)}) %collective-permute-start) | collective-permute-done | bytes 65568 | tf_op jit(solution)/shard_map/ppermute | solution.py:244
  12.7 3.1 %collective-permute-start.1 = (f32[128,128]{1,0:T(8,128)S(1)}, f32[128,128]{1,0:T(8,128)S(1)}, u32[]{:S(2)}, u32[]{:S(2)}) collective-permute-start(f32[128,128]{1,0:T(8,128)S(1)} %add.64), channel_id=1, source_target_pairs={{0,2},{1,3},{2,0},{3,1},{4,6},{5,7},{6,4},{7,5},{8,10},{9,11},{10,... | collective-permute-start | bytes 196616 | tf_op jit(solution)/shard_map/ppermute | solution.py:244
  15.8 2.2 %collective-permute-done.1 = f32[128,128]{1,0:T(8,128)S(1)} collective-permute-done((f32[128,128]{1,0:T(8,128)S(1)}, f32[128,128]{1,0:T(8,128)S(1)}, u32[]{:S(2)}, u32[]{:S(2)}) %collective-permute-start.1) | collective-permute-done | bytes 65568 | tf_op jit(solution)/shard_map/ppermute | solution.py:244
  18.1 1.2 collective-permute-done.2
  19.4 1.9 %collective-permute-start.3 = (f32[128,128]{1,0:T(8,128)S(1)}, f32[128,128]{1,0:T(8,128)S(1)}, u32[]{:S(2)}, u32[]{:S(2)}) collective-permute-start(f32[128,128]{1,0:T(8,128)S(1)} %add.66), channel_id=1, source_target_pairs={{0,8},{1,9},{2,10},{3,11},{4,12},{5,13},{6,14},{7,15},{8,0},{9,1},... | collective-permute-start | bytes 196616 | tf_op jit(solution)/shard_map/ppermute | solution.py:244
  21.3 2.4 %collective-permute-done.3 = f32[128,128]{1,0:T(8,128)S(1)} collective-permute-done((f32[128,128]{1,0:T(8,128)S(1)}, f32[128,128]{1,0:T(8,128)S(1)}, u32[]{:S(2)}, u32[]{:S(2)}) %collective-permute-start.3) | collective-permute-done | bytes 65568 | tf_op jit(solution)/shard_map/ppermute | solution.py:244
  23.7 1.9 %collective-permute-start.4 = (f32[128,128]{1,0:T(8,128)S(1)}, f32[128,128]{1,0:T(8,128)S(1)}, u32[]{:S(2)}, u32[]{:S(2)}) collective-permute-start(f32[128,128]{1,0:T(8,128)S(1)} %add.67), channel_id=1, source_target_pairs={{0,16},{1,17},{2,18},{3,19},{4,20},{5,21},{6,22},{7,23},{8,24},{9,... | collective-permute-start | bytes 196616 | tf_op jit(solution)/shard_map/ppermute | solution.py:244
  25.7 0.7 copy.10.restart_ref
  26.4 1.7 %collective-permute-done.4 = f32[128,128]{1,0:T(8,128)S(1)} collective-permute-done((f32[128,128]{1,0:T(8,128)S(1)}, f32[128,128]{1,0:T(8,128)S(1)}, u32[]{:S(2)}, u32[]{:S(2)}) %collective-permute-start.4) | collective-permute-done | bytes 65568 | tf_op jit(solution)/shard_map/ppermute | solution.py:244
  28.7 11.3 %update.1 = (f32[32,168,128]{2,1,0:T(8,128)}, f32[128,40]{1,0:T(8,128)S(1)}) custom-call(f32[128,128]{1,0:T(8,128)} %add.68.s_ref, f32[120,40]{1,0:T(8,128)} %copy.10.restart_ref, f32[120,16384]{1,0:T(8,128)} %u_hbm.3, f32[1,16384]{1,0:T(1,128)} %r_hbm.3), custom_call_target="tpu_custom_call" | custom-call | tf_op jit(solution)/shard_map/update/pallas_call | solution.py:174
  40.0 6.8 %all-to-all-start = ((f32[32,168,128]{2,1,0:T(8,128)}), f32[32,168,128]{2,1,0:T(8,128)S(1)}, u32[]{:S(2)}, u32[]{:S(2)}) async-start(f32[32,168,128]{2,1,0:T(8,128)} %get-tuple-element.7), calls=%async_computation | async-start | bytes 5505024 | tf_op jit(solution)/shard_map/all_to_all | solution.py:271
  47.1 1.8 %collective-permute-start.5 = (f32[3,40,30]{1,2,0:T(8,128)S(1)}, f32[3,40,30]{1,2,0:T(8,128)S(1)}, u32[]{:S(2)}, u32[]{:S(2)}) collective-permute-start(f32[3,40,30]{1,2,0:T(8,128)S(1)} %convolution_bitcast_fusion), channel_id=1, source_target_pairs={{0,1},{1,2},{2,3},{3,0},{4,5},{5,6},{6,7},{7,4},{8,9},{9,10},{10,1... | collective-permute-start | bytes 43208 | tf_op jit(solution)/shard_map/ppermute | solution.py:251
  48.9 2.4 %collective-permute-start.6 = (f32[3,40,30]{1,2,0:T(8,128)S(1)}, f32[3,40,30]{1,2,0:T(8,128)S(1)}, u32[]{:S(2)}, u32[]{:S(2)}) collective-permute-start(f32[3,40,30]{1,2,0:T(8,128)S(1)} %convolution_bitcast_fusion), channel_id=1, source_target_pairs={{0,2},{1,3},{2,0},{3,1},{4,6},{5,7},{6,4},{7,5},{8,10},{9,11},{10,... | collective-permute-start | bytes 43208 | tf_op jit(solution)/shard_map/ppermute | solution.py:251
  51.4 1.4 %collective-permute-start.7 = (f32[3,40,30]{1,2,0:T(8,128)S(1)}, f32[3,40,30]{1,2,0:T(8,128)S(1)}, u32[]{:S(2)}, u32[]{:S(2)}) collective-permute-start(f32[3,40,30]{1,2,0:T(8,128)S(1)} %convolution_bitcast_fusion), channel_id=1, source_target_pairs={{0,3},{1,0},{2,1},{3,2},{4,7},{5,4},{6,5},{7,6},{8,11},{9,8},{10,9... | collective-permute-start | bytes 43208 | tf_op jit(solution)/shard_map/ppermute | solution.py:251
  52.8 0.7 fusion.3
  53.5 44.9 %collective-permute-done.5 = f32[3,40,30]{1,2,0:T(8,128)S(1)} collective-permute-done((f32[3,40,30]{1,2,0:T(8,128)S(1)}, f32[3,40,30]{1,2,0:T(8,128)S(1)}, u32[]{:S(2)}, u32[]{:S(2)}) %collective-permute-start.5) | collective-permute-done | bytes 14432 | tf_op jit(solution)/shard_map/ppermute | solution.py:251
  98.4 16.0 %collective-permute-done.6 = f32[3,40,30]{1,2,0:T(8,128)S(1)} collective-permute-done((f32[3,40,30]{1,2,0:T(8,128)S(1)}, f32[3,40,30]{1,2,0:T(8,128)S(1)}, u32[]{:S(2)}, u32[]{:S(2)}) %collective-permute-start.6) | collective-permute-done | bytes 14432 | tf_op jit(solution)/shard_map/ppermute | solution.py:251
  114.4 2.6 %add_bitcast_fusion.2 = f32[1,3,40,30]{2,3,1,0:T(8,128)S(1)} fusion(f32[3,40,30]{1,2,0:T(8,128)S(1)} %collective-permute-done.7, f32[3,40,30]{1,2,0:T(8,128)S(1)} %collective-permute-done.6, f32[3,40,30]{1,2,0:T(8,128)S(1)} %collective-permute-done.5, f32[3,40,30]{1,2,0:T(8,128)S(1)} %convolution_bitcast_fusion, pred[]{:T(512)} %bitcast.10, pred[]{:T(512)} %bitcast.9, ...), kind=kLoop, calls=%fused_computation.8 | loop fusion | flops 25200 | bytes 72004 | tf_op jit(solution)/shard_map/stack | solution.py:254
  117.0 7.5 %add_bitcast_fusion.3 = (f32[1,3,40,30]{2,3,1,0:T(8,128)S(1)}, f32[1,3,40,30]{2,3,1,0:T(8,128)S(1)}, f32[1,3,40,30]{2,3,1,0:T(8,128)S(1)}) fusion(f32[3,40,30]{1,2,0:T(8,128)S(1)} %collective-permute-done.7, f32[3,40,30]{1,2,0:T(8,128)S(1)} %collective-permute-done.6, f32[3,40,30]{1,2,0:T(8,128)S(1)} %collective-permute-done.5, ...), kind=kLoop, calls=%fused_computation.9 | loop fusion | flops 75600 | bytes 100812 | tf_op jit(solution)/shard_map/stack | solution.py:254
  124.5 0.7 multiply_reduce_fusion
  126.1 0.8 mul.21
  126.9 2.6 %settle.1 = (f32[40,16384]{1,0:T(8,128)}, f32[1,16384]{1,0:T(1,128)}) custom-call(s32[1,32]{1,0:T(1,128)S(1)} %copy-done.1, f32[32,168,128]{2,1,0:T(8,128)S(1)} %all-to-all-done.got_ref), custom_call_target="tpu_custom_call" | custom-call | tf_op jit(solution)/shard_map/settle/pallas_call | solution.py:225
  (19 shorter events, 1.2 us)
Async XLA Ops:
  0.6 46.3 %copy-start = (f32[3,120,30]{1,2,0:T(8,128)S(1)}, f32[3,120,30]{1,2,0:T(8,128)}, u32[]{:S(2)}) copy-start(f32[3,120,30]{1,2,0:T(8,128)} %param.9) | copy-start | bytes 129604
  0.6 25.0 %copy-start.2 = (f32[120,40]{0,1:T(8,128)S(1)}, f32[120,40]{0,1:T(8,128)}, u32[]{:S(2)}) copy-start(f32[120,40]{0,1:T(8,128)} %param.8) | copy-start | bytes 57604
  7.3 5.4 %collective-permute-start = (f32[128,128]{1,0:T(8,128)S(1)}, f32[128,128]{1,0:T(8,128)S(1)}, u32[]{:S(2)}, u32[]{:S(2)}) collective-permute-start(f32[128,128]{1,0:T(8,128)S(1)} %gram.1), channel_id=1, source_target_pairs={{0,1},{1,0},{2,3},{3,2},{4,5},{5,4},{6,7},{7,6},{8,9},{9,8},{10,11... | collective-permute-start | bytes 196616 | tf_op jit(solution)/shard_map/ppermute | solution.py:244
  12.7 5.3 %collective-permute-start.1 = (f32[128,128]{1,0:T(8,128)S(1)}, f32[128,128]{1,0:T(8,128)S(1)}, u32[]{:S(2)}, u32[]{:S(2)}) collective-permute-start(f32[128,128]{1,0:T(8,128)S(1)} %add.64), channel_id=1, source_target_pairs={{0,2},{1,3},{2,0},{3,1},{4,6},{5,7},{6,4},{7,5},{8,10},{9,11},{10,... | collective-permute-start | bytes 196616 | tf_op jit(solution)/shard_map/ppermute | solution.py:244
  18.1 1.3 %collective-permute-start.2 = (f32[128,128]{1,0:T(8,128)S(1)}, f32[128,128]{1,0:T(8,128)S(1)}, u32[]{:S(2)}, u32[]{:S(2)}) collective-permute-start(f32[128,128]{1,0:T(8,128)S(1)} %add.65), channel_id=1, source_target_pairs={{0,4},{1,5},{2,6},{3,7},{4,0},{5,1},{6,2},{7,3},{8,12},{9,13},{10,... | collective-permute-start | bytes 196616 | tf_op jit(solution)/shard_map/ppermute | solution.py:244
  19.4 4.3 %collective-permute-start.3 = (f32[128,128]{1,0:T(8,128)S(1)}, f32[128,128]{1,0:T(8,128)S(1)}, u32[]{:S(2)}, u32[]{:S(2)}) collective-permute-start(f32[128,128]{1,0:T(8,128)S(1)} %add.66), channel_id=1, source_target_pairs={{0,8},{1,9},{2,10},{3,11},{4,12},{5,13},{6,14},{7,15},{8,0},{9,1},... | collective-permute-start | bytes 196616 | tf_op jit(solution)/shard_map/ppermute | solution.py:244
  23.7 4.3 %collective-permute-start.4 = (f32[128,128]{1,0:T(8,128)S(1)}, f32[128,128]{1,0:T(8,128)S(1)}, u32[]{:S(2)}, u32[]{:S(2)}) collective-permute-start(f32[128,128]{1,0:T(8,128)S(1)} %add.67), channel_id=1, source_target_pairs={{0,16},{1,17},{2,18},{3,19},{4,20},{5,21},{6,22},{7,23},{8,24},{9,... | collective-permute-start | bytes 196616 | tf_op jit(solution)/shard_map/ppermute | solution.py:244
  40.0 86.8 %copy-start.1 = (s32[1,32]{1,0:T(1,128)S(1)}, s32[1,32]{1,0:T(1,128)}, u32[]{:S(2)}) copy-start(s32[1,32]{1,0:T(1,128)} %slot_ref.1) | copy-start | bytes 388
  40.0 86.8 %all-to-all-start = ((f32[32,168,128]{2,1,0:T(8,128)}), f32[32,168,128]{2,1,0:T(8,128)S(1)}, u32[]{:S(2)}, u32[]{:S(2)}) async-start(f32[32,168,128]{2,1,0:T(8,128)} %get-tuple-element.7), calls=%async_computation | async-start | bytes 5505024 | tf_op jit(solution)/shard_map/all_to_all | solution.py:271
  47.1 51.3 %collective-permute-start.5 = (f32[3,40,30]{1,2,0:T(8,128)S(1)}, f32[3,40,30]{1,2,0:T(8,128)S(1)}, u32[]{:S(2)}, u32[]{:S(2)}) collective-permute-start(f32[3,40,30]{1,2,0:T(8,128)S(1)} %convolution_bitcast_fusion), channel_id=1, source_target_pairs={{0,1},{1,2},{2,3},{3,0},{4,5},{5,6},{6,7},{7,4},{8,9},{9,10},{10,1... | collective-permute-start | bytes 43208 | tf_op jit(solution)/shard_map/ppermute | solution.py:251
  48.9 65.4 %collective-permute-start.6 = (f32[3,40,30]{1,2,0:T(8,128)S(1)}, f32[3,40,30]{1,2,0:T(8,128)S(1)}, u32[]{:S(2)}, u32[]{:S(2)}) collective-permute-start(f32[3,40,30]{1,2,0:T(8,128)S(1)} %convolution_bitcast_fusion), channel_id=1, source_target_pairs={{0,2},{1,3},{2,0},{3,1},{4,6},{5,7},{6,4},{7,5},{8,10},{9,11},{10,... | collective-permute-start | bytes 43208 | tf_op jit(solution)/shard_map/ppermute | solution.py:251
  51.4 63.0 %collective-permute-start.7 = (f32[3,40,30]{1,2,0:T(8,128)S(1)}, f32[3,40,30]{1,2,0:T(8,128)S(1)}, u32[]{:S(2)}, u32[]{:S(2)}) collective-permute-start(f32[3,40,30]{1,2,0:T(8,128)S(1)} %convolution_bitcast_fusion), channel_id=1, source_target_pairs={{0,3},{1,0},{2,1},{3,2},{4,7},{5,4},{6,5},{7,6},{8,11},{9,8},{10,9... | collective-permute-start | bytes 43208 | tf_op jit(solution)/shard_map/ppermute | solution.py:251

commit v3 on v2

--- a/solution.py
+++ b/solution.py
@@ -246,16 +246,6 @@
     return x
 
 
-def gather_sub(x):
-    nsub = lax.axis_size("sub")
-    turns = [x] + [lax.ppermute(x, "sub", [(i, (i + d) % nsub) for i in range(nsub)]) for d in range(1, nsub)]
-    order = (lax.axis_index("sub") - jnp.arange(nsub)) % nsub
-    picks = jax.nn.one_hot(order, nsub, dtype=jnp.bool_)
-    return jnp.stack(
-        [functools.reduce(lambda a, b: a + b, [jnp.where(picks[t, d], turns[d], 0.0) for d in range(nsub)]) for t in range(nsub)]
-    )
-
-
 def local(u_fem, resid_fem, slot_map, restart, coeff):
     ndev = lax.axis_size(AXES)
     k, n = u_fem.shape
@@ -265,14 +255,16 @@
     chunks = block // LANES
     tile = block * max(1, min(ndev, 2048 // block))
 
+    nsub = lax.axis_size("sub")
+    coeff_all = lax.all_to_all(jnp.broadcast_to(coeff[None], (nsub,) + coeff.shape), "sub", 0, 0, tiled=True)
     whole = total_of(gram_call(u_fem, resid_fem, tile), ndev)
     height = -(-(chunks * (keep + 1) + 1) // 8) * 8
     sent, raised = update_call(whole, restart, u_fem, resid_fem, ndev, float(nrows), block, height, tile)
     got = lax.all_to_all(sent, AXES, 0, 0, tiled=True)
     new_rows, next_row = settle_call(slot_map, got, keep, block, float(nrows))
 
-    rotated = jnp.einsum("kp,ikm->ipm", raised[:k], coeff, precision=HIGH)
-    rotated = jnp.moveaxis(gather_sub(rotated), 0, 2).reshape(coeff.shape[0], keep, -1)
+    coeff_all = jnp.moveaxis(coeff_all, 0, 2).reshape(coeff.shape[0], k, -1)
+    rotated = jnp.einsum("kp,ikm->ipm", raised[:k], coeff_all, precision=HIGH)
     new_coeff = rotated * lax.rsqrt(jnp.mean(rotated * rotated) + 1e-06)
     return (new_rows, next_row, new_coeff)
 

time: 130 us -> 113 us (0.87)
  other arithmetic: 11.6 us -> 1.31 us
  starting transfers between devices: 22.5 us -> 18.8 us
  waiting for transfers between devices: 70.8 us -> 67.3 us
    ppermute x3 -> x0, waiting for transfers between devices: 60.9 us -> none  [gather_sub(): lax.ppermute(x, 'sub', [(i, (i + d) % nsub) for i in range(nsub)])]
    all_to_all x1, waiting for transfers between devices: 0.01 us -> 59 us  [local(): got = lax.all_to_all(sent, AXES, 0, 0, tiled=True)]
    another operation x2 -> x0, other arithmetic: 10.1 us -> none  [gather_sub(): jnp.stack([functools.reduce(lambda a, b: a + b, [jnp.where(picks[t, d], t...]
    ppermute x3 -> x0, starting transfers between devices: 5.65 us -> none  [gather_sub(): lax.ppermute(x, 'sub', [(i, (i + d) % nsub) for i in range(nsub)])]
    all_to_all x0 -> x1, starting transfers between devices: none -> 3.37 us  [local(): lax.all_to_all(jnp.broadcast_to(coeff[None], (nsub,) + coeff.shape), 'sub...]
    ppermute x5, waiting for transfers between devices: 9.87 us -> 8.28 us  [total_of(): x = x + lax.ppermute(x, AXES, [(i, i ^ bit) for i in range(ndev)])]
  transfers between devices with their start and end apart: 9 -> 7, of which waited for: 7 -> 5; matrix products, arithmetic and copies ran while one was open for 10% -> 3% of each run, Pallas kernels for 0% -> 10%
where the time goes in v3:
time: 113 us; the launch traced here: 112 us
  waiting for transfers between devices  67.3 us (60%)
  Pallas kernels  20.6 us (18%)
  starting transfers between devices  18.8 us (17%)
  local copies, waits for them, and re-layouts  1.46 us (1%)
  between operations  1.45 us (1%)
  other arithmetic  1.31 us (1%)
    all_to_all x1, waiting for transfers between devices, local(): got = lax.all_to_all(sent, AXES, 0, 0, tiled=True)  59 us
    pallas_call x1, Pallas kernels, update_call(): pl.pallas_call(functools.partial(update_body, nrows=nrows, block=block, t...  11.3 us
    ppermute x5, starting transfers between devices, total_of(): x = x + lax.ppermute(x, AXES, [(i, i ^ bit) for i in range(ndev)])  9.43 us
    ppermute x5, waiting for transfers between devices, total_of(): x = x + lax.ppermute(x, AXES, [(i, i ^ bit) for i in range(ndev)])  8.28 us
    pallas_call x1, Pallas kernels, gram_call(): pl.pallas_call(functools.partial(gram_body, tile=tile), in_specs=[far, fa...  6.66 us
    all_to_all x1, starting transfers between devices, local(): got = lax.all_to_all(sent, AXES, 0, 0, tiled=True)  6.03 us
    all_to_all x1, starting transfers between devices, local(): lax.all_to_all(jnp.broadcast_to(coeff[None], (nsub,) + coeff.shape), 'sub...  3.37 us
    pallas_call x1, Pallas kernels, settle_call(): pl.pallas_call(functools.partial(settle_body, keep=keep, block=block, nro...  2.61 us
  transfers between devices with their start and end apart: 7, of which 5 were waited for; matrix products, arithmetic and copies ran while one was open for 3% of the time, Pallas kernels for 10%

profile of v3, /device:TPU:0, one launch (start us, length us, event | category | flops | bytes accessed | tf_op | source)
XLA Modules:
  0.0 112.0 jit_solution(15890638369460790920)
XLA Ops:
  0.7 6.7 %gram.1 = f32[128,128]{1,0:T(8,128)S(1)} custom-call(f32[120,16384]{1,0:T(8,128)} %u_hbm.3, f32[1,16384]{1,0:T(1,128)} %r_hbm.3), custom_call_target="tpu_custom_call" | custom-call | tf_op jit(solution)/shard_map/gram/pallas_call | solution.py:51
  7.3 3.1 %collective-permute-start = (f32[128,128]{1,0:T(8,128)S(1)}, f32[128,128]{1,0:T(8,128)S(1)}, u32[]{:S(2)}, u32[]{:S(2)}) collective-permute-start(f32[128,128]{1,0:T(8,128)S(1)} %gram.1), channel_id=1, source_target_pairs={{0,1},{1,0},{2,3},{3,2},{4,5},{5,4},{6,7},{7,6},{8,9},{9,8},{10,11... | collective-permute-start | bytes 196616 | tf_op jit(solution)/shard_map/ppermute | solution.py:244
  10.4 2.2 %collective-permute-done = f32[128,128]{1,0:T(8,128)S(1)} collective-permute-done((f32[128,128]{1,0:T(8,128)S(1)}, f32[128,128]{1,0:T(8,128)S(1)}, u32[]{:S(2)}, u32[]{:S(2)}) %collective-permute-start) | collective-permute-done | bytes 65568 | tf_op jit(solution)/shard_map/ppermute | solution.py:244
  12.7 3.1 %collective-permute-start.1 = (f32[128,128]{1,0:T(8,128)S(1)}, f32[128,128]{1,0:T(8,128)S(1)}, u32[]{:S(2)}, u32[]{:S(2)}) collective-permute-start(f32[128,128]{1,0:T(8,128)S(1)} %add.18), channel_id=1, source_target_pairs={{0,2},{1,3},{2,0},{3,1},{4,6},{5,7},{6,4},{7,5},{8,10},{9,11},{10,... | collective-permute-start | bytes 196616 | tf_op jit(solution)/shard_map/ppermute | solution.py:244
  15.8 0.0 copy-done.1
  15.8 0.7 broadcast_in_dim.2
  16.5 3.4 %all-to-all-start.1 = ((f32[4,3,120,30]{2,3,1,0:T(8,128)}), f32[4,3,120,30]{2,3,1,0:T(8,128)S(1)}, u32[]{:S(2)}, u32[]{:S(2)}) async-start(f32[4,3,120,30]{2,3,1,0:T(8,128)} %broadcast_in_dim.2), calls=%async_computation.1 | async-start | bytes 393216 | tf_op jit(solution)/shard_map/all_to_all | solution.py:259
  19.9 0.0 collective-permute-done.1
  19.9 0.1 collective-permute-start.2
  20.0 1.2 %collective-permute-done.2 = f32[128,128]{1,0:T(8,128)S(1)} collective-permute-done((f32[128,128]{1,0:T(8,128)S(1)}, f32[128,128]{1,0:T(8,128)S(1)}, u32[]{:S(2)}, u32[]{:S(2)}) %collective-permute-start.2) | collective-permute-done | bytes 65568 | tf_op jit(solution)/shard_map/ppermute | solution.py:244
  21.2 1.6 %collective-permute-start.3 = (f32[128,128]{1,0:T(8,128)S(1)}, f32[128,128]{1,0:T(8,128)S(1)}, u32[]{:S(2)}, u32[]{:S(2)}) collective-permute-start(f32[128,128]{1,0:T(8,128)S(1)} %add.20), channel_id=1, source_target_pairs={{0,8},{1,9},{2,10},{3,11},{4,12},{5,13},{6,14},{7,15},{8,0},{9,1},... | collective-permute-start | bytes 196616 | tf_op jit(solution)/shard_map/ppermute | solution.py:244
  22.8 2.8 %collective-permute-done.3 = f32[128,128]{1,0:T(8,128)S(1)} collective-permute-done((f32[128,128]{1,0:T(8,128)S(1)}, f32[128,128]{1,0:T(8,128)S(1)}, u32[]{:S(2)}, u32[]{:S(2)}) %collective-permute-start.3) | collective-permute-done | bytes 65568 | tf_op jit(solution)/shard_map/ppermute | solution.py:244
  25.6 1.6 %collective-permute-start.4 = (f32[128,128]{1,0:T(8,128)S(1)}, f32[128,128]{1,0:T(8,128)S(1)}, u32[]{:S(2)}, u32[]{:S(2)}) collective-permute-start(f32[128,128]{1,0:T(8,128)S(1)} %add.21), channel_id=1, source_target_pairs={{0,16},{1,17},{2,18},{3,19},{4,20},{5,21},{6,22},{7,23},{8,24},{9,... | collective-permute-start | bytes 196616 | tf_op jit(solution)/shard_map/ppermute | solution.py:244
  27.2 0.7 copy.14.restart_ref
  27.9 2.0 %collective-permute-done.4 = f32[128,128]{1,0:T(8,128)S(1)} collective-permute-done((f32[128,128]{1,0:T(8,128)S(1)}, f32[128,128]{1,0:T(8,128)S(1)}, u32[]{:S(2)}, u32[]{:S(2)}) %collective-permute-start.4) | collective-permute-done | bytes 65568 | tf_op jit(solution)/shard_map/ppermute | solution.py:244
  29.9 0.6 add.22.s_ref
  30.5 11.3 %update.1 = (f32[32,168,128]{2,1,0:T(8,128)}, f32[128,40]{1,0:T(8,128)S(1)}) custom-call(f32[128,128]{1,0:T(8,128)} %add.22.s_ref, f32[120,40]{1,0:T(8,128)} %copy.14.restart_ref, f32[120,16384]{1,0:T(8,128)} %u_hbm.3, f32[1,16384]{1,0:T(1,128)} %r_hbm.3), custom_call_target="tpu_custom_call" | custom-call | tf_op jit(solution)/shard_map/update/pallas_call | solution.py:174
  41.9 0.0 all-to-all-done.1
  41.9 0.0 copy-start
  41.9 6.0 %all-to-all-start = ((f32[32,168,128]{2,1,0:T(8,128)}), f32[32,168,128]{2,1,0:T(8,128)S(1)}, u32[]{:S(2)}, u32[]{:S(2)}) async-start(f32[32,168,128]{2,1,0:T(8,128)} %get-tuple-element.7), calls=%async_computation | async-start | bytes 5505024 | tf_op jit(solution)/shard_map/all_to_all | solution.py:263
  48.0 1.1 multiply_reduce_fusion
  49.8 0.6 multiply_bitcast_fusion
  50.4 59.0 %all-to-all-done.got_ref = f32[32,168,128]{2,1,0:T(8,128)S(1)} async-done(((f32[32,168,128]{2,1,0:T(8,128)}), f32[32,168,128]{2,1,0:T(8,128)S(1)}, u32[]{:S(2)}, u32[]{:S(2)}) %all-to-all-start) | async-done | bytes 2752544 | tf_op jit(solution)/shard_map/all_to_all | solution.py:263
  109.4 2.6 %settle.1 = (f32[40,16384]{1,0:T(8,128)}, f32[1,16384]{1,0:T(1,128)}) custom-call(s32[1,32]{1,0:T(1,128)S(1)} %copy-done, f32[32,168,128]{2,1,0:T(8,128)S(1)} %all-to-all-done.got_ref), custom_call_target="tpu_custom_call" | custom-call | tf_op jit(solution)/shard_map/settle/pallas_call | solution.py:225
  (10 shorter events, 0.1 us)
Async XLA Ops:
  0.6 15.2 %copy-start.1 = (f32[3,120,30]{1,2,0:T(8,128)S(1)}, f32[3,120,30]{1,2,0:T(8,128)}, u32[]{:S(2)}) copy-start(f32[3,120,30]{1,2,0:T(8,128)} %param.9) | copy-start | bytes 129604
  0.6 26.5 %copy-start.2 = (f32[120,40]{0,1:T(8,128)S(1)}, f32[120,40]{0,1:T(8,128)}, u32[]{:S(2)}) copy-start(f32[120,40]{0,1:T(8,128)} %param.8) | copy-start | bytes 57604
  7.3 5.4 %collective-permute-start = (f32[128,128]{1,0:T(8,128)S(1)}, f32[128,128]{1,0:T(8,128)S(1)}, u32[]{:S(2)}, u32[]{:S(2)}) collective-permute-start(f32[128,128]{1,0:T(8,128)S(1)} %gram.1), channel_id=1, source_target_pairs={{0,1},{1,0},{2,3},{3,2},{4,5},{5,4},{6,7},{7,6},{8,9},{9,8},{10,11... | collective-permute-start | bytes 196616 | tf_op jit(solution)/shard_map/ppermute | solution.py:244
  12.7 7.2 %collective-permute-start.1 = (f32[128,128]{1,0:T(8,128)S(1)}, f32[128,128]{1,0:T(8,128)S(1)}, u32[]{:S(2)}, u32[]{:S(2)}) collective-permute-start(f32[128,128]{1,0:T(8,128)S(1)} %add.18), channel_id=1, source_target_pairs={{0,2},{1,3},{2,0},{3,1},{4,6},{5,7},{6,4},{7,5},{8,10},{9,11},{10,... | collective-permute-start | bytes 196616 | tf_op jit(solution)/shard_map/ppermute | solution.py:244
  16.5 25.4 %all-to-all-start.1 = ((f32[4,3,120,30]{2,3,1,0:T(8,128)}), f32[4,3,120,30]{2,3,1,0:T(8,128)S(1)}, u32[]{:S(2)}, u32[]{:S(2)}) async-start(f32[4,3,120,30]{2,3,1,0:T(8,128)} %broadcast_in_dim.2), calls=%async_computation.1 | async-start | bytes 393216 | tf_op jit(solution)/shard_map/all_to_all | solution.py:259
  19.9 1.3 %collective-permute-start.2 = (f32[128,128]{1,0:T(8,128)S(1)}, f32[128,128]{1,0:T(8,128)S(1)}, u32[]{:S(2)}, u32[]{:S(2)}) collective-permute-start(f32[128,128]{1,0:T(8,128)S(1)} %add.19), channel_id=1, source_target_pairs={{0,4},{1,5},{2,6},{3,7},{4,0},{5,1},{6,2},{7,3},{8,12},{9,13},{10,... | collective-permute-start | bytes 196616 | tf_op jit(solution)/shard_map/ppermute | solution.py:244
  21.2 4.3 %collective-permute-start.3 = (f32[128,128]{1,0:T(8,128)S(1)}, f32[128,128]{1,0:T(8,128)S(1)}, u32[]{:S(2)}, u32[]{:S(2)}) collective-permute-start(f32[128,128]{1,0:T(8,128)S(1)} %add.20), channel_id=1, source_target_pairs={{0,8},{1,9},{2,10},{3,11},{4,12},{5,13},{6,14},{7,15},{8,0},{9,1},... | collective-permute-start | bytes 196616 | tf_op jit(solution)/shard_map/ppermute | solution.py:244
  25.6 4.3 %collective-permute-start.4 = (f32[128,128]{1,0:T(8,128)S(1)}, f32[128,128]{1,0:T(8,128)S(1)}, u32[]{:S(2)}, u32[]{:S(2)}) collective-permute-start(f32[128,128]{1,0:T(8,128)S(1)} %add.21), channel_id=1, source_target_pairs={{0,16},{1,17},{2,18},{3,19},{4,20},{5,21},{6,22},{7,23},{8,24},{9,... | collective-permute-start | bytes 196616 | tf_op jit(solution)/shard_map/ppermute | solution.py:244
  41.9 67.5 %copy-start = (s32[1,32]{1,0:T(1,128)S(1)}, s32[1,32]{1,0:T(1,128)}, u32[]{:S(2)}) copy-start(s32[1,32]{1,0:T(1,128)} %slot_ref.1) | copy-start | bytes 388
  41.9 67.5 %all-to-all-start = ((f32[32,168,128]{2,1,0:T(8,128)}), f32[32,168,128]{2,1,0:T(8,128)S(1)}, u32[]{:S(2)}, u32[]{:S(2)}) async-start(f32[32,168,128]{2,1,0:T(8,128)} %get-tuple-element.7), calls=%async_computation | async-start | bytes 5505024 | tf_op jit(solution)/shard_map/all_to_all | solution.py:263
